TPU v7x, 32 devices: a whole 2x2x4 slice. The times are simulated.
32 devices in a mesh: gx: 4 (over x, core), gy: 8 (over z, y).
Axes of the slice: x: 2, y: 2, z: 4, core: 2. Of those that a mesh axis runs over, the one named last changes fastest.
Arguments:
- hot_ids: int32 [262144], P(('gx', 'gy')), may hold values from 0 to 2047
- hot_grads: bfloat16 [262144, 128], P(('gx', 'gy')), may hold values from -6 to 6
- cold_grads: bfloat16 [4, 8, 8, 512, 128], P('gx', 'gy'), may hold values from -6 to 6
- cold_slots: int32 [4, 8, 8, 512], P('gx', 'gy'), may hold values from 0 to 2047
- cold_counts: int32 [4, 8, 8], P('gx', 'gy'), may hold values from 1 to 512, as said below
Outputs:
- hot_grad: float32 [2048, 128], replicated
- cold_grad: float32 [4, 16384, 128], P('gx', 'gy')
Inputs may be any that keep to these rules, and one draw needn't show every extreme that they name: In each group g, some owner d receives cold_counts[g, s, d] = 512 from every s; loads per owner are skewed.
All inputs are finite; a program needn't handle non-finite values.
Results may differ from a plain program's by a relative error of at most 0.0003.
Values may be sent and summed in bfloat16 or wider, within the bound.
A program may use at most 64 MiB of HBM per device.

v0:
```python
import math
import jax
import jax.numpy as jnp
from jax import lax
from jax.sharding import PartitionSpec as P

HOT = 2048
OWN_ROWS = 2048


def onehot_sum(row_ids, row_data, table_size, block_rows):
    turns = row_ids.shape[0] // block_rows
    id_blocks = row_ids.reshape(turns, block_rows)
    data_blocks = row_data.reshape(turns, block_rows, row_data.shape[1])
    table_iota = lax.broadcasted_iota(jnp.int32, (table_size, block_rows), 0)

    def add_block(total, pieces):
        ids_here, data_here = pieces
        selector = (table_iota == ids_here[None, :]).astype(jnp.bfloat16)
        return (total + jnp.dot(selector, data_here, preferred_element_type=jnp.float32), None)

    start = jnp.zeros((table_size, row_data.shape[1]), jnp.float32)
    total, unused = lax.scan(add_block, start, (id_blocks, data_blocks))
    return total


def hot_part(hot_ids, hot_grads):
    hot_rows = HOT
    block_rows = math.gcd(hot_ids.shape[0], 2048)
    local_sum = onehot_sum(hot_ids, hot_grads, hot_rows, block_rows)
    factor = (hot_rows / (hot_ids.shape[0] * lax.axis_size("gx") * lax.axis_size("gy"))) ** 0.5
    shared = lax.psum_scatter(local_sum, "gy", scatter_dimension=0, tiled=True)
    shared = lax.psum(shared, "gx")
    total = lax.all_gather(shared, "gy", axis=0, tiled=True)
    return total * factor


def cold_part(cold_grads, cold_slots, cold_counts):
    owners, capacity, width = (cold_grads.shape[2], cold_grads.shape[3], cold_grads.shape[4])
    grads_here = cold_grads.reshape(owners, capacity, width)
    slots_here = cold_slots.reshape(owners, capacity)
    counts_here = cold_counts.reshape(owners)
    places = lax.broadcasted_iota(jnp.int32, (owners, capacity), 1)
    valid = places < counts_here[:, None]
    payload = jnp.where(valid[:, :, None], grads_here, jnp.zeros_like(grads_here))
    got_rows, got_slots = (
        lax.all_to_all(payload, "gy", split_axis=0, concat_axis=0, tiled=True),
        lax.all_to_all(slots_here, "gy", split_axis=0, concat_axis=0, tiled=True),
    )
    total_rows = owners * capacity
    block_rows = math.gcd(total_rows, 1024)
    table = onehot_sum(
        got_slots.reshape(total_rows), got_rows.reshape(total_rows, width), OWN_ROWS, block_rows
    )
    return table.reshape(1, OWN_ROWS, width)


def per_device(hot_ids, hot_grads, cold_grads, cold_slots, cold_counts):
    hot_grad = hot_part(hot_ids, hot_grads)
    cold_grad = cold_part(cold_grads, cold_slots, cold_counts)
    return (hot_grad, cold_grad)


def solution(mesh):
    return jax.shard_map(
        per_device,
        mesh=mesh,
        in_specs=(
            P(("gx", "gy")),
            P(("gx", "gy"), None),
            P("gx", "gy", None, None, None),
            P("gx", "gy", None, None),
            P("gx", "gy", None),
        ),
        out_specs=(P(), P("gx", "gy", None)),
        check_vma=False,
    )
```

profile of v0, /device:TPU:0, one launch (start us, length us, event | category | flops | bytes accessed | tf_op | source)
XLA Modules:
  0.0 185.8 jit_solution(4274179711939193013)
XLA Ops:
  7.2 0.0 reduce-scatter.2.cloned.1.call-start
  7.2 0.8 reshape.43
  8.0 0.0 copy-start.2
  8.0 0.0 copy-start.3
  8.0 0.0 copy-start
  8.0 17.7 %while.22 = (s32[]{:T(128)}, f32[2048,128]{1,0:T(8,128)S(1)}, s32[4,2048]{1,0:T(4,128)S(1)}, bf16[4,2048,128]{2,1,0:T(8,128)(2,1)}, s32[]{:T(128)}, /*index=5*/s32[]{:T(128)}) while((s32[]{:T(128)}, f32[2048,128]{1,0:T(8,128)S(1)}, s32[4,2048]{1,0:T(4,128)S(1)}, bf16[4,2048,128]{2,1,0:T(8,128)(2,1)}, s32[]{:T(128)}, ...), condition=%wide.region_1.2_spmd.clone, body=%wide.region_0.1_spmd.clone.sunk | while | flops 1078460416 | bytes 2646611 | solution.py:23
  8.1 4.4 %fusion.21 = f32[2048,128]{1,0:T(8,128)S(1)} fusion(s32[2048]{0:T(1024)S(1)} %bitcast.25, f32[2048,128]{1,0:T(8,128)S(1)} %get-tuple-element.165, bf16[4,2048,128]{2,1,0:T(8,128)(2,1)} %get-tuple-element.173, s32[]{:T(128)} %get-tuple-element.164, pred[]{:T(512)S(6)} %compare.6), kind=kOutput, calls=%fused_computation.5.clone.1 | convolution fusion | flops 1078460416 | bytes 2630145 | tf_op jit(solution)/shard_map/while/body/eval_jaxpr/dot_general | solution.py:20
  12.6 4.4 %fusion.21 = f32[2048,128]{1,0:T(8,128)S(1)} fusion(s32[2048]{0:T(1024)S(1)} %bitcast.25, f32[2048,128]{1,0:T(8,128)S(1)} %get-tuple-element.165, bf16[4,2048,128]{2,1,0:T(8,128)(2,1)} %get-tuple-element.173, s32[]{:T(128)} %get-tuple-element.164, pred[]{:T(512)S(6)} %compare.6), kind=kOutput, calls=%fused_computation.5.clone.1 | convolution fusion | flops 1078460416 | bytes 2630145 | tf_op jit(solution)/shard_map/while/body/eval_jaxpr/dot_general | solution.py:20
  17.0 4.4 %fusion.21 = f32[2048,128]{1,0:T(8,128)S(1)} fusion(s32[2048]{0:T(1024)S(1)} %bitcast.25, f32[2048,128]{1,0:T(8,128)S(1)} %get-tuple-element.165, bf16[4,2048,128]{2,1,0:T(8,128)(2,1)} %get-tuple-element.173, s32[]{:T(128)} %get-tuple-element.164, pred[]{:T(512)S(6)} %compare.6), kind=kOutput, calls=%fused_computation.5.clone.1 | convolution fusion | flops 1078460416 | bytes 2630145 | tf_op jit(solution)/shard_map/while/body/eval_jaxpr/dot_general | solution.py:20
  21.4 4.4 %fusion.21 = f32[2048,128]{1,0:T(8,128)S(1)} fusion(s32[2048]{0:T(1024)S(1)} %bitcast.25, f32[2048,128]{1,0:T(8,128)S(1)} %get-tuple-element.165, bf16[4,2048,128]{2,1,0:T(8,128)(2,1)} %get-tuple-element.173, s32[]{:T(128)} %get-tuple-element.164, pred[]{:T(512)S(6)} %compare.6), kind=kOutput, calls=%fused_computation.5.clone.1 | convolution fusion | flops 1078460416 | bytes 2630145 | tf_op jit(solution)/shard_map/while/body/eval_jaxpr/dot_general | solution.py:20
  25.7 0.0 copy-start.1
  25.8 1.0 copy-done.1
  26.7 0.0 reduce-scatter.2.cloned.1.call-update
  26.7 0.0 copy-done.2
  26.8 0.6 all_to_all.9
  27.4 7.3 %all-to-all-start = ((s32[8,1,512]{2,1,0:T(1,128)}), s32[8,1,512]{2,1,0:T(1,128)S(1)}, u32[]{:S(2)}, u32[]{:S(2)}) async-start(s32[8,1,512]{2,1,0:T(1,128)} %all_to_all.9), calls=%async_computation.1 | async-start | bytes 32768 | tf_op jit(solution)/shard_map/all_to_all | solution.py:48
  34.7 0.0 copy-done.3
  34.7 0.1 iota_compare_fusion.8
  34.8 0.0 copy-done
  34.8 1.5 bitcast_select_fusion
  36.2 5.1 %all-to-all-done = s32[8,1,512]{2,1,0:T(1,128)S(1)} async-done(((s32[8,1,512]{2,1,0:T(1,128)}), s32[8,1,512]{2,1,0:T(1,128)S(1)}, u32[]{:S(2)}, u32[]{:S(2)}) %all-to-all-start) | async-done | bytes 16416 | tf_op jit(solution)/shard_map/all_to_all | solution.py:48
  41.3 3.6 %all-to-all-start.1 = ((bf16[8,512,128]{2,1,0:T(8,128)(2,1)}), bf16[8,512,128]{2,1,0:T(8,128)(2,1)S(1)}, u32[]{:S(2)}, u32[]{:S(2)}) async-start(bf16[8,512,128]{2,1,0:T(8,128)(2,1)} %bitcast_select_fusion), calls=%async_computation.2 | async-start | bytes 2097152 | tf_op jit(solution)/shard_map/all_to_all | solution.py:47
  44.9 0.0 all-reduce.2.cloned.1.call-start
  44.9 56.6 %reduce-scatter.2.cloned.1.call-done = f32[256,128]{1,0:T(8,128)} async-done(((f32[2048,128]{1,0:T(8,128)}), f32[256,128]{1,0:T(8,128)}) %reduce-scatter.2.cloned.1.call-update) | async-done | bytes 131088 | tf_op jit(solution)/shard_map/reduce_scatter | solution.py:32
  101.6 0.0 all-reduce.2.cloned.1.call-update
  101.6 0.0 all-gather.2.cloned.1.call-start
  101.6 32.9 %all-reduce.2.cloned.1.call-done = f32[256,128]{1,0:T(8,128)} async-done(((f32[256,128]{1,0:T(8,128)}), f32[256,128]{1,0:T(8,128)}) %all-reduce.2.cloned.1.call-update) | async-done | bytes 131088 | tf_op jit(solution)/shard_map/psum | solution.py:33
  134.6 0.0 all-gather.2.cloned.1.call-update
  134.7 0.0 all-to-all-done.1
  134.7 7.3 %while.23 = (s32[]{:T(128)}, f32[2048,128]{1,0:T(8,128)S(1)}, s32[4,1024]{1,0:T(4,128)S(1)}, bf16[4,1024,128]{2,1,0:T(8,128)(2,1)S(1)}, s32[]{:T(128)}, /*index=5*/s32[]{:T(128)}) while((s32[]{:T(128)}, f32[2048,128]{1,0:T(8,128)S(1)}, s32[4,1024]{1,0:T(4,128)S(1)}, bf16[4,1024,128]{2,1,0:T(8,128)(2,1)S(1)}, s32[]{:T(128)}, ...), condition=%wide.region_5.6_spmd.clone, body=%wide.region_4.5_spmd.clone.sunk | while | flops 539492352 | bytes 2371671 | solution.py:23
  134.7 1.8 fusion.23
  136.5 1.8 fusion.23
  138.4 1.8 fusion.23
  140.2 1.8 fusion.23
  142.0 0.0 copy-start.4
  142.0 35.0 %all-gather.2.cloned.1.call-done = f32[2048,128]{1,0:T(8,128)} async-done(((f32[256,128]{1,0:T(8,128)}), f32[2048,128]{1,0:T(8,128)}) %all-gather.2.cloned.1.call-update) | async-done | bytes 1048592 | tf_op jit(solution)/shard_map/all_gather | solution.py:34
  177.0 2.3 %broadcast_multiply_fusion = f32[2048,128]{1,0:T(8,128)} fusion(f32[2048,128]{1,0:T(8,128)} %all-gather.2.cloned.1.call-done), kind=kLoop, calls=%fused_computation.19 | loop fusion | flops 262144 | bytes 2097152 | tf_op jit(solution)/shard_map/mul | solution.py:35
  179.3 0.0 copy-done.4
  (12 shorter events, 0.1 us)
Async XLA Ops:
  7.2 94.4 %reduce-scatter.2.cloned.1.call-start = ((), (), s32[]{:S(2)}) async-start(), calls=%async_computation.3 | async-start | bytes 1179648 | tf_op jit(solution)/shard_map/reduce_scatter | solution.py:32
  8.0 18.8 %copy-start.2 = (s32[1,1,8,512]{3,2,1,0:T(8,128)S(1)}, s32[1,1,8,512]{3,2,1,0:T(8,128)}, u32[]{:S(2)}) copy-start(s32[1,1,8,512]{3,2,1,0:T(8,128)} %param.12) | copy-start | bytes 49156
  8.0 26.7 %copy-start.3 = (s32[1,1,8]{2,1,0:T(1,128)S(1)}, s32[1,1,8]{2,1,0:T(1,128)}, u32[]{:S(2)}) copy-start(s32[1,1,8]{2,1,0:T(1,128)} %param.13) | copy-start | bytes 100
  8.0 26.7 %copy-start = (bf16[1,1,8,512,128]{4,3,2,1,0:T(8,128)(2,1)S(1)}, bf16[1,1,8,512,128]{4,3,2,1,0:T(8,128)(2,1)}, u32[]{:S(2)}) copy-start(bf16[1,1,8,512,128]{4,3,2,1,0:T(8,128)(2,1)} %param.11) | copy-start | bytes 3145732
  25.7 1.0 copy-start.1
  27.4 13.9 %all-to-all-start = ((s32[8,1,512]{2,1,0:T(1,128)}), s32[8,1,512]{2,1,0:T(1,128)S(1)}, u32[]{:S(2)}, u32[]{:S(2)}) async-start(s32[8,1,512]{2,1,0:T(1,128)} %all_to_all.9), calls=%async_computation.1 | async-start | bytes 32768 | tf_op jit(solution)/shard_map/all_to_all | solution.py:48
  41.3 93.4 %all-to-all-start.1 = ((bf16[8,512,128]{2,1,0:T(8,128)(2,1)}), bf16[8,512,128]{2,1,0:T(8,128)(2,1)S(1)}, u32[]{:S(2)}, u32[]{:S(2)}) async-start(bf16[8,512,128]{2,1,0:T(8,128)(2,1)} %bitcast_select_fusion), calls=%async_computation.2 | async-start | bytes 2097152 | tf_op jit(solution)/shard_map/all_to_all | solution.py:47
  44.9 89.7 %all-reduce.2.cloned.1.call-start = ((), (), s32[]{:S(2)}) async-start(), calls=%async_computation.4 | async-start | bytes 262144 | tf_op jit(solution)/shard_map/psum | solution.py:33
  101.6 75.4 %all-gather.2.cloned.1.call-start = ((), (), s32[]{:S(2)}) async-start(), calls=%async_computation.5 | async-start | bytes 1179648 | tf_op jit(solution)/shard_map/all_gather | solution.py:34
  142.0 37.3 %copy-start.4 = (f32[2048,128]{1,0:T(8,128)}, f32[2048,128]{1,0:T(8,128)S(1)}, u32[]{:S(2)}) copy-start(f32[2048,128]{1,0:T(8,128)S(1)} %get-tuple-element.57) | copy-start | bytes 3145732
Sparse Core Ops, SparseCore 0:
  26.9 74.6 reduce-scatter.1
  103.9 30.6 all-reduce.1
  136.7 40.2 all-gather.1
where the time goes:
time: 186 us
  waiting for transfers between devices  130 us (70%)
  matrix products  24.7 us (13%)
  between operations  13.9 us (7%)
  starting transfers between devices  11 us (6%)
  other arithmetic  3.89 us (2%)
  local copies, waits for them, and re-layouts  2.47 us (1%)
    reduce_scatter x1, waiting for transfers between devices, hot_part(): shared = lax.psum_scatter(local_sum, 'gy', scatter_dimension=0, tiled=True)  56.6 us
    all_gather x1, waiting for transfers between devices, hot_part(): total = lax.all_gather(shared, 'gy', axis=0, tiled=True)  35 us
    psum x1, waiting for transfers between devices, hot_part(): shared = lax.psum(shared, 'gx')  32.9 us
    dot_general x8, matrix products, add_block(): jnp.dot(selector, data_here, preferred_element_type=jnp.float32)  24.7 us
    all_to_all x1, starting transfers between devices, cold_part(): lax.all_to_all(slots_here, 'gy', split_axis=0, concat_axis=0, tiled=True)  7.31 us
    all_to_all x1, waiting for transfers between devices, cold_part(): lax.all_to_all(slots_here, 'gy', split_axis=0, concat_axis=0, tiled=True)  5.07 us
  transfers between devices with their start and end apart: 5, of which 4 were waited for; matrix products, arithmetic and copies ran while one was open for 5% of the time, Pallas kernels for 0%

commit v1 on v0

--- a/solution.py
+++ b/solution.py
@@ -30,7 +30,7 @@
     local_sum = onehot_sum(hot_ids, hot_grads, hot_rows, block_rows)
     factor = (hot_rows / (hot_ids.shape[0] * lax.axis_size("gx") * lax.axis_size("gy"))) ** 0.5
     shared = lax.psum_scatter(local_sum, "gy", scatter_dimension=0, tiled=True)
-    shared = lax.psum(shared, "gx")
+    shared = jnp.sum(lax.all_gather(shared, "gx"), axis=0)
     total = lax.all_gather(shared, "gy", axis=0, tiled=True)
     return total * factor
 

time: 186 us -> 158 us (0.85)
  waiting for transfers between devices: 130 us -> 93 us
  blocking collectives: 0 us -> 7.33 us
    psum x1 -> x0, waiting for transfers between devices: 32.9 us -> none  [hot_part(): shared = lax.psum(shared, 'gx')]
    all_gather x0 -> x1, blocking collectives: none -> 7.33 us  [hot_part(): shared = jnp.sum(lax.all_gather(shared, 'gx'), axis=0)]
    all_gather x1, waiting for transfers between devices: 35 us -> 31.3 us  [hot_part(): total = lax.all_gather(shared, 'gy', axis=0, tiled=True)]
  transfers between devices with their start and end apart: 5 -> 4, of which waited for: 4 -> 3; matrix products, arithmetic and copies ran while one was open for 5% -> 6% of each run, Pallas kernels for 0% -> 0%
where the time goes in v1:
time: 158 us; the launch traced here: 157 us
  waiting for transfers between devices  93 us (59%)
  matrix products  24.7 us (16%)
  between operations  14.2 us (9%)
  starting transfers between devices  10.9 us (7%)
  blocking collectives  7.33 us (5%)
  other arithmetic  4.57 us (3%)
  local copies, waits for them, and re-layouts  2.47 us (2%)
    reduce_scatter x1, waiting for transfers between devices, hot_part(): shared = lax.psum_scatter(local_sum, 'gy', scatter_dimension=0, tiled=True)  56.6 us
    all_gather x1, waiting for transfers between devices, hot_part(): total = lax.all_gather(shared, 'gy', axis=0, tiled=True)  31.3 us
    dot_general x8, matrix products, add_block(): jnp.dot(selector, data_here, preferred_element_type=jnp.float32)  24.7 us
    all_gather x1, blocking collectives, hot_part(): shared = jnp.sum(lax.all_gather(shared, 'gx'), axis=0)  7.33 us
    all_to_all x1, starting transfers between devices, cold_part(): lax.all_to_all(slots_here, 'gy', split_axis=0, concat_axis=0, tiled=True)  7.31 us
    all_to_all x1, waiting for transfers between devices, cold_part(): lax.all_to_all(slots_here, 'gy', split_axis=0, concat_axis=0, tiled=True)  5.07 us
    all_to_all x1, starting transfers between devices, cold_part(): lax.all_to_all(payload, 'gy', split_axis=0, concat_axis=0, tiled=True)  3.56 us
  transfers between devices with their start and end apart: 4, of which 3 were waited for; matrix products, arithmetic and copies ran while one was open for 6% of the time, Pallas kernels for 0%

profile of v1, /device:TPU:0, one launch (start us, length us, event | category | flops | bytes accessed | tf_op | source)
XLA Modules:
  0.0 157.4 jit_solution(13209905520132617439)
XLA Ops:
  7.2 0.0 reduce-scatter.2.cloned.1.call-start
  7.2 0.8 reshape.43
  8.0 0.0 copy-start.2
  8.0 0.0 copy-start.3
  8.0 0.0 copy-start
  8.0 17.7 %while.22 = (s32[]{:T(128)}, f32[2048,128]{1,0:T(8,128)S(1)}, s32[4,2048]{1,0:T(4,128)S(1)}, bf16[4,2048,128]{2,1,0:T(8,128)(2,1)}, s32[]{:T(128)}, /*index=5*/s32[]{:T(128)}) while((s32[]{:T(128)}, f32[2048,128]{1,0:T(8,128)S(1)}, s32[4,2048]{1,0:T(4,128)S(1)}, bf16[4,2048,128]{2,1,0:T(8,128)(2,1)}, s32[]{:T(128)}, ...), condition=%wide.region_1.2_spmd.clone, body=%wide.region_0.1_spmd.clone.sunk | while | flops 1078460416 | bytes 2646111 | solution.py:23
  8.1 4.4 %fusion.21 = f32[2048,128]{1,0:T(8,128)S(1)} fusion(s32[2048]{0:T(1024)S(1)} %bitcast.27, f32[2048,128]{1,0:T(8,128)S(1)} %get-tuple-element.165, bf16[4,2048,128]{2,1,0:T(8,128)(2,1)} %get-tuple-element.173, s32[]{:T(128)S(6)} %copy.9, pred[]{:T(512)S(6)} %compare.6), kind=kOutput, calls=%fused_computation.5.clone.1 | convolution fusion | flops 1078460416 | bytes 2629637 | tf_op jit(solution)/shard_map/while/body/eval_jaxpr/dot_general | solution.py:20
  12.6 4.4 %fusion.21 = f32[2048,128]{1,0:T(8,128)S(1)} fusion(s32[2048]{0:T(1024)S(1)} %bitcast.27, f32[2048,128]{1,0:T(8,128)S(1)} %get-tuple-element.165, bf16[4,2048,128]{2,1,0:T(8,128)(2,1)} %get-tuple-element.173, s32[]{:T(128)S(6)} %copy.9, pred[]{:T(512)S(6)} %compare.6), kind=kOutput, calls=%fused_computation.5.clone.1 | convolution fusion | flops 1078460416 | bytes 2629637 | tf_op jit(solution)/shard_map/while/body/eval_jaxpr/dot_general | solution.py:20
  17.0 4.4 %fusion.21 = f32[2048,128]{1,0:T(8,128)S(1)} fusion(s32[2048]{0:T(1024)S(1)} %bitcast.27, f32[2048,128]{1,0:T(8,128)S(1)} %get-tuple-element.165, bf16[4,2048,128]{2,1,0:T(8,128)(2,1)} %get-tuple-element.173, s32[]{:T(128)S(6)} %copy.9, pred[]{:T(512)S(6)} %compare.6), kind=kOutput, calls=%fused_computation.5.clone.1 | convolution fusion | flops 1078460416 | bytes 2629637 | tf_op jit(solution)/shard_map/while/body/eval_jaxpr/dot_general | solution.py:20
  21.4 4.4 %fusion.21 = f32[2048,128]{1,0:T(8,128)S(1)} fusion(s32[2048]{0:T(1024)S(1)} %bitcast.27, f32[2048,128]{1,0:T(8,128)S(1)} %get-tuple-element.165, bf16[4,2048,128]{2,1,0:T(8,128)(2,1)} %get-tuple-element.173, s32[]{:T(128)S(6)} %copy.9, pred[]{:T(512)S(6)} %compare.6), kind=kOutput, calls=%fused_computation.5.clone.1 | convolution fusion | flops 1078460416 | bytes 2629637 | tf_op jit(solution)/shard_map/while/body/eval_jaxpr/dot_general | solution.py:20
  25.8 0.0 copy-start.1
  25.8 1.0 copy-done.1
  26.7 0.0 reduce-scatter.2.cloned.1.call-update
  26.8 0.0 copy-done.2
  26.8 0.6 all_to_all.9
  27.4 7.3 %all-to-all-start = ((s32[8,1,512]{2,1,0:T(1,128)}), s32[8,1,512]{2,1,0:T(1,128)S(1)}, u32[]{:S(2)}, u32[]{:S(2)}) async-start(s32[8,1,512]{2,1,0:T(1,128)} %all_to_all.9), calls=%async_computation.1 | async-start | bytes 32768 | tf_op jit(solution)/shard_map/all_to_all | solution.py:48
  34.7 0.0 copy-done.3
  34.7 0.1 iota_compare_fusion.8
  34.8 0.0 copy-done
  34.8 1.5 bitcast_select_fusion
  36.2 5.1 %all-to-all-done = s32[8,1,512]{2,1,0:T(1,128)S(1)} async-done(((s32[8,1,512]{2,1,0:T(1,128)}), s32[8,1,512]{2,1,0:T(1,128)S(1)}, u32[]{:S(2)}, u32[]{:S(2)}) %all-to-all-start) | async-done | bytes 16416 | tf_op jit(solution)/shard_map/all_to_all | solution.py:48
  41.3 3.6 %all-to-all-start.1 = ((bf16[8,512,128]{2,1,0:T(8,128)(2,1)}), bf16[8,512,128]{2,1,0:T(8,128)(2,1)S(1)}, u32[]{:S(2)}, u32[]{:S(2)}) async-start(bf16[8,512,128]{2,1,0:T(8,128)(2,1)} %bitcast_select_fusion), calls=%async_computation.2 | async-start | bytes 2097152 | tf_op jit(solution)/shard_map/all_to_all | solution.py:47
  44.9 0.0 all-gather.3.cloned.1.call-start
  44.9 56.6 %reduce-scatter.2.cloned.1.call-done = f32[256,128]{1,0:T(8,128)} async-done(((f32[2048,128]{1,0:T(8,128)}), f32[256,128]{1,0:T(8,128)}) %reduce-scatter.2.cloned.1.call-update) | async-done | bytes 131088 | tf_op jit(solution)/shard_map/reduce_scatter | solution.py:32
  101.6 7.3 %all-gather = f32[1024,128]{1,0:T(8,128)S(1)} all-gather(f32[256,128]{1,0:T(8,128)} %reduce-scatter.2.cloned.1.call-done), channel_id=2, replica_groups=mesh['gx'=4,'gy'=8] {'gx'}, dimensions={0}, use_global_device_ids=true | all-gather | bytes 655360 | tf_op jit(solution)/shard_map/all_gather | solution.py:33
  108.9 0.7 reduce_sum.9
  109.6 0.0 all-gather.3.cloned.1.call-update
  109.7 0.0 all-to-all-done.1
  109.7 7.3 %while.23 = (s32[]{:T(128)}, f32[2048,128]{1,0:T(8,128)S(1)}, s32[4,1024]{1,0:T(4,128)S(1)}, bf16[4,1024,128]{2,1,0:T(8,128)(2,1)S(1)}, s32[]{:T(128)}, /*index=5*/s32[]{:T(128)}) while((s32[]{:T(128)}, f32[2048,128]{1,0:T(8,128)S(1)}, s32[4,1024]{1,0:T(4,128)S(1)}, bf16[4,1024,128]{2,1,0:T(8,128)(2,1)S(1)}, s32[]{:T(128)}, ...), condition=%wide.region_5.6_spmd.clone, body=%wide.region_4.5_spmd.clone.sunk | while | flops 539492352 | bytes 2371679 | solution.py:23
  109.7 1.8 %fusion.23 = f32[2048,128]{1,0:T(8,128)S(1)} fusion(s32[1024]{0:T(1024)S(1)} %bitcast.28, f32[2048,128]{1,0:T(8,128)S(1)} %get-tuple-element.183, pred[]{:T(512)S(6)} %compare.7, bf16[4,1024,128]{2,1,0:T(8,128)(2,1)S(1)} %get-tuple-element.191, s32[]{:T(128)S(6)} %copy.15), kind=kOutput, calls=%fused_computation.13.clone.1 | convolution fusion | flops 539492352 | bytes 2363397 | tf_op jit(solution)/shard_map/while/body/eval_jaxpr/dot_general | solution.py:20
  111.5 1.8 %fusion.23 = f32[2048,128]{1,0:T(8,128)S(1)} fusion(s32[1024]{0:T(1024)S(1)} %bitcast.28, f32[2048,128]{1,0:T(8,128)S(1)} %get-tuple-element.183, pred[]{:T(512)S(6)} %compare.7, bf16[4,1024,128]{2,1,0:T(8,128)(2,1)S(1)} %get-tuple-element.191, s32[]{:T(128)S(6)} %copy.15), kind=kOutput, calls=%fused_computation.13.clone.1 | convolution fusion | flops 539492352 | bytes 2363397 | tf_op jit(solution)/shard_map/while/body/eval_jaxpr/dot_general | solution.py:20
  113.4 1.8 %fusion.23 = f32[2048,128]{1,0:T(8,128)S(1)} fusion(s32[1024]{0:T(1024)S(1)} %bitcast.28, f32[2048,128]{1,0:T(8,128)S(1)} %get-tuple-element.183, pred[]{:T(512)S(6)} %compare.7, bf16[4,1024,128]{2,1,0:T(8,128)(2,1)S(1)} %get-tuple-element.191, s32[]{:T(128)S(6)} %copy.15), kind=kOutput, calls=%fused_computation.13.clone.1 | convolution fusion | flops 539492352 | bytes 2363397 | tf_op jit(solution)/shard_map/while/body/eval_jaxpr/dot_general | solution.py:20
  115.2 1.8 %fusion.23 = f32[2048,128]{1,0:T(8,128)S(1)} fusion(s32[1024]{0:T(1024)S(1)} %bitcast.28, f32[2048,128]{1,0:T(8,128)S(1)} %get-tuple-element.183, pred[]{:T(512)S(6)} %compare.7, bf16[4,1024,128]{2,1,0:T(8,128)(2,1)S(1)} %get-tuple-element.191, s32[]{:T(128)S(6)} %copy.15), kind=kOutput, calls=%fused_computation.13.clone.1 | convolution fusion | flops 539492352 | bytes 2363397 | tf_op jit(solution)/shard_map/while/body/eval_jaxpr/dot_general | solution.py:20
  117.0 0.0 copy-start.4
  117.0 31.3 %all-gather.3.cloned.1.call-done = f32[2048,128]{1,0:T(8,128)} async-done(((f32[256,128]{1,0:T(8,128)}), f32[2048,128]{1,0:T(8,128)}) %all-gather.3.cloned.1.call-update) | async-done | bytes 1048592 | tf_op jit(solution)/shard_map/all_gather | solution.py:34
  148.3 2.3 %broadcast_multiply_fusion = f32[2048,128]{1,0:T(8,128)} fusion(f32[2048,128]{1,0:T(8,128)} %all-gather.3.cloned.1.call-done), kind=kLoop, calls=%fused_computation.19 | loop fusion | flops 262144 | bytes 2097152 | tf_op jit(solution)/shard_map/mul | solution.py:35
  150.6 0.0 copy-done.4
  (12 shorter events, 0.1 us)
Async XLA Ops:
  7.2 94.4 %reduce-scatter.2.cloned.1.call-start = ((), (), s32[]{:S(2)}) async-start(), calls=%async_computation.3 | async-start | bytes 1179648 | tf_op jit(solution)/shard_map/reduce_scatter | solution.py:32
  8.0 18.8 %copy-start.2 = (s32[1,1,8,512]{3,2,1,0:T(8,128)S(1)}, s32[1,1,8,512]{3,2,1,0:T(8,128)}, u32[]{:S(2)}) copy-start(s32[1,1,8,512]{3,2,1,0:T(8,128)} %param.12) | copy-start | bytes 49156
  8.0 26.7 %copy-start.3 = (s32[1,1,8]{2,1,0:T(1,128)S(1)}, s32[1,1,8]{2,1,0:T(1,128)}, u32[]{:S(2)}) copy-start(s32[1,1,8]{2,1,0:T(1,128)} %param.13) | copy-start | bytes 100
  8.0 26.7 %copy-start = (bf16[1,1,8,512,128]{4,3,2,1,0:T(8,128)(2,1)S(1)}, bf16[1,1,8,512,128]{4,3,2,1,0:T(8,128)(2,1)}, u32[]{:S(2)}) copy-start(bf16[1,1,8,512,128]{4,3,2,1,0:T(8,128)(2,1)} %param.11) | copy-start | bytes 3145732
  25.8 1.0 copy-start.1
  27.4 13.9 %all-to-all-start = ((s32[8,1,512]{2,1,0:T(1,128)}), s32[8,1,512]{2,1,0:T(1,128)S(1)}, u32[]{:S(2)}, u32[]{:S(2)}) async-start(s32[8,1,512]{2,1,0:T(1,128)} %all_to_all.9), calls=%async_computation.1 | async-start | bytes 32768 | tf_op jit(solution)/shard_map/all_to_all | solution.py:48
  41.3 68.4 %all-to-all-start.1 = ((bf16[8,512,128]{2,1,0:T(8,128)(2,1)}), bf16[8,512,128]{2,1,0:T(8,128)(2,1)S(1)}, u32[]{:S(2)}, u32[]{:S(2)}) async-start(bf16[8,512,128]{2,1,0:T(8,128)(2,1)} %bitcast_select_fusion), calls=%async_computation.2 | async-start | bytes 2097152 | tf_op jit(solution)/shard_map/all_to_all | solution.py:47
  44.9 103.4 %all-gather.3.cloned.1.call-start = ((), (), s32[]{:S(2)}) async-start(), calls=%async_computation.4 | async-start | bytes 1179648 | tf_op jit(solution)/shard_map/all_gather | solution.py:34
  117.0 33.6 %copy-start.4 = (f32[2048,128]{1,0:T(8,128)}, f32[2048,128]{1,0:T(8,128)S(1)}, u32[]{:S(2)}) copy-start(f32[2048,128]{1,0:T(8,128)S(1)} %get-tuple-element.57) | copy-start | bytes 3145732
Sparse Core Ops, SparseCore 0:
  26.9 74.6 reduce-scatter.1
  109.7 38.5 all-gather.2
